TPU v7x, 32 devices: a whole 2x2x4 slice. The times are simulated.
32 devices in a mesh: dp: 8 (over z, x), feat: 4 (over y, core).
Axes of the slice: x: 2, y: 2, z: 4, core: 2. Of those that a mesh axis runs over, the one named last changes fastest.
Arguments:
- activations: bfloat16 [2048, 8192], P('dp', 'feat'), may hold values from -6 to 6
- cotangent: bfloat16 [2048, 1024], P('dp'), may hold values from -0.13183594 to 0.13183594
- weight: float32 [8192, 1024], P('feat'), may hold values from -0.0625 to 0.0625
- stats_old: float32 [4, 8, 4, 256, 256], P('feat', 'dp'), as said below
- owners: int32 [32, 4], replicated, may hold values from 0 to 7, as said below
- next_acts: bfloat16 [2048, 8192], P('dp', 'feat'), may hold values from -6 to 6
Outputs:
- weight_new: float32 [8192, 1024], P('feat')
- stats_new: float32 [4, 8, 4, 256, 256], P('feat', 'dp')
- next_out: bfloat16 [2048, 1024], P('dp', 'feat')
Inputs may be any that keep to these rules, and one draw needn't show every extreme that they name: `owners`: blocks are grouped by the index of feat that holds their rows (8192 / (256 * 4) row blocks a group); in every group each dp index owns at most 4 blocks, and some dp index owns exactly 4. `stats_old`: every slot holds a symmetric positive definite matrix; slots that no block maps to are not read.
All inputs are finite; a program needn't handle non-finite values.
Results may differ from a plain program's by a relative error of at most 0.02.
Values may be sent and summed in bfloat16 or wider, within the bound.
A program may use at most 128 MiB of HBM per device.

v0:
```python
import jax
import jax.numpy as jnp
from jax import lax
from jax.sharding import PartitionSpec as P

ITERS = 6
decay_rate = 0.9
step_rate = 0.01


def from_root(x, axis, root):
    mine = lax.axis_index(axis) == root
    return lax.psum(jnp.where(mine, x, jnp.zeros_like(x)), axis)


def newton_root(stats):
    width = stats.shape[0]
    identity = jnp.eye(width, dtype=jnp.float32)
    norm_value = jnp.sqrt(jnp.sum(stats * stats) + 1e-06)
    matrix = stats / norm_value
    iterate = identity
    for counter in range(ITERS):
        factor = (5.0 * identity - matrix) / 4.0
        factor_low = factor.astype(jnp.bfloat16)
        iterate = jnp.dot(
            iterate.astype(jnp.bfloat16), factor_low, preferred_element_type=jnp.float32
        )
        if counter + 1 < ITERS:
            square = jnp.dot(factor_low, factor_low, preferred_element_type=jnp.float32).astype(
                jnp.bfloat16
            )
            fourth = jnp.dot(square, square, preferred_element_type=jnp.float32).astype(
                jnp.bfloat16
            )
            matrix = jnp.dot(
                fourth, matrix.astype(jnp.bfloat16), preferred_element_type=jnp.float32
            )
    return iterate * norm_value ** (-0.25)


def update_stats(grad_block, old_stats):
    gram = (
        jnp.dot(grad_block, grad_block.T, preferred_element_type=jnp.float32) / grad_block.shape[0]
    )
    return decay_rate * old_stats + (1.0 - decay_rate) * gram


def block_at(matrix, block_id, col_blocks, width):
    row_start = block_id // col_blocks * width
    col_start = block_id % col_blocks * width
    return lax.dynamic_slice(matrix, (row_start, col_start), (width, width))


def body(activations, cotangent, weight, stats_old, owners, next_acts):
    width = stats_old.shape[-1]
    slots = stats_old.shape[2]
    rows_dev, columns = weight.shape
    row_blocks = rows_dev // width
    col_blocks = columns // width
    block_count = row_blocks * col_blocks
    partial_grad = jnp.einsum(
        "td,tc->dc", activations, cotangent, preferred_element_type=jnp.float32
    )
    summed = lax.psum(partial_grad, "dp")
    grad_low = summed.astype(jnp.bfloat16)
    feat_index = lax.axis_index("feat")
    data_index = lax.axis_index("dp")
    own_list = lax.dynamic_slice_in_dim(owners, feat_index * row_blocks, row_blocks, 0).reshape(
        block_count
    )
    is_mine = (own_list == data_index).astype(jnp.int32)
    slot_of = jnp.cumsum(is_mine) - is_mine
    block_ids = jnp.arange(block_count, dtype=jnp.int32)
    slot_pick = jnp.clip(slot_of, 0, slots - 1)
    stats_list = []
    renewed_list = []
    chosen_list = []
    for position in range(slots):
        picked = (is_mine == 1) & (slot_of == position)
        alive = jnp.any(picked)
        chosen = jnp.sum(jnp.where(picked, block_ids, 0))
        grad_block = block_at(grad_low, chosen, col_blocks, width)
        renewed = update_stats(grad_block, stats_old[0, 0, position])
        stats_list.append(jnp.where(alive, renewed, 0.0))
        renewed_list.append(renewed)
        chosen_list.append(chosen)
    root_list = [newton_root(renewed) for renewed in renewed_list]
    new_list = []
    fresh_list = []
    for root_matrix, chosen in zip(root_list, chosen_list):
        grad_block = block_at(grad_low, chosen, col_blocks, width)
        weight_block = block_at(weight, chosen, col_blocks, width)
        update = jnp.dot(
            root_matrix.astype(jnp.bfloat16), grad_block, preferred_element_type=jnp.float32
        )
        fresh_list.append(weight_block - step_rate * update)
    candidates = jnp.stack(fresh_list)
    for position in range(block_count):
        sending = lax.dynamic_index_in_dim(candidates, slot_pick[position], 0, keepdims=False)
        new_list.append(
            from_root(sending.astype(jnp.bfloat16), "dp", own_list[position]).astype(sending.dtype)
        )
    new_blocks = jnp.stack(new_list)
    weight_new = (
        new_blocks.reshape(row_blocks, col_blocks, width, width)
        .transpose(0, 2, 1, 3)
        .reshape(rows_dev, columns)
    )
    stats_out = jnp.stack(stats_list)[None, None]
    partial_next = jnp.dot(
        next_acts, weight_new.astype(jnp.bfloat16), preferred_element_type=jnp.float32
    )
    next_out = lax.psum_scatter(
        partial_next.astype(jnp.bfloat16), "feat", scatter_dimension=1, tiled=True
    )
    return (weight_new, stats_out, next_out)


def solution(mesh):
    placed = (
        P("dp", "feat"),
        P("dp", None),
        P("feat", None),
        P("feat", "dp", None, None, None),
        P(),
        P("dp", "feat"),
    )
    return jax.shard_map(
        body,
        mesh=mesh,
        in_specs=placed,
        out_specs=(P("feat", None), P("feat", "dp", None, None, None), P("dp", "feat")),
        check_vma=False,
    )
```

profile of v0, /device:TPU:0, one launch (start us, length us, event | category | flops | bytes accessed | tf_op | source)
XLA Modules:
  0.0 700.2 jit_solution(15082206161460627291)
XLA Ops:
  7.2 0.8 constant_dynamic-slice_fusion
  8.5 0.7 fusion.355
  9.2 0.7 fusion.356
  9.9 0.6 select_reduce_fusion
  13.1 5.7 fusion.363
  18.9 328.1 %all-reduce.5 = bf16[2048,1024]{1,0:T(8,128)(2,1)} all-reduce(f32[2048,1024]{1,0:T(8,128)} %fusion.363), channel_id=1, replica_groups=mesh['dp'=8,'feat'=4] {'dp'}, use_global_device_ids=true, to_apply=%region_2.3 | all-reduce | flops 2097152 | bytes 12582912 | tf_op jit(solution)/shard_map/psum | solution.py:64
  347.0 1.8 multiply_reduce_fusion
  349.5 0.7 select_bitcast_fusion
  350.2 0.4 convolution_convert_fusion.13
  351.3 1.0 convolution_convert_fusion.12
  354.6 1.9 multiply_reduce_fusion.1
  357.1 0.7 select_bitcast_fusion.1
  357.8 0.4 convolution_convert_fusion.28
  358.5 0.4 convolution_convert_fusion.25
  358.9 1.0 convolution_convert_fusion.27
  360.0 0.6 select_reduce_fusion.2
  363.3 1.9 multiply_reduce_fusion.2
  365.8 0.6 select_bitcast_fusion.2
  367.6 1.0 convolution_convert_fusion.42
  370.9 1.8 multiply_reduce_fusion.3
  373.3 0.7 select_bitcast_fusion.3
  375.2 1.0 convolution_convert_fusion.57
  376.3 0.7 fusion.362
  378.3 0.7 fusion.361
  384.1 0.7 fusion.360
  386.3 0.7 fusion.359
  419.8 0.4 convolution_convert_fusion.7
  421.7 1.2 convolution_convert_fusion.6
  423.1 0.4 convolution_convert_fusion.22
  425.8 1.2 fusion.2
  427.4 1.2 fusion.6
  428.8 0.4 convolution_convert_fusion.37
  430.1 0.4 convolution_convert_fusion.31
  431.4 1.2 fusion.10
  435.5 1.2 fusion.14
  476.9 0.8 fusion.69
  477.7 1.0 fusion.78
  478.8 1.1 fusion.87
  479.8 1.1 fusion.96
  481.2 166.1 %all-reduce.4.cloned.1.call-done = (bf16[1,256,256]{2,1,0:T(8,128)(2,1)}, bf16[1,256,256]{2,1,0:T(8,128)(2,1)}, bf16[1,256,256]{2,1,0:T(8,128)(2,1)}, bf16[1,256...) async-done(((bf16[1,256,256]{2,1,0:T(8,128)(2,1)}, ...) | async-done | bytes 4194320 | tf_op jit(solution)/shard_map/psum | solution.py:13
  647.4 1.1 constant_dynamic-update-slice_fusion.31
  648.5 0.9 constant_dynamic-update-slice_fusion.30
  649.4 0.9 constant_dynamic-update-slice_fusion.29
  650.3 0.9 constant_dynamic-update-slice_fusion.28
  651.3 0.9 constant_dynamic-update-slice_fusion.27
  652.2 0.9 constant_dynamic-update-slice_fusion.26
  653.1 0.9 constant_dynamic-update-slice_fusion.25
  654.0 0.9 constant_dynamic-update-slice_fusion.24
  654.9 0.9 constant_dynamic-update-slice_fusion.23
  655.9 0.9 constant_dynamic-update-slice_fusion.22
  656.8 0.9 constant_dynamic-update-slice_fusion.21
  657.7 0.9 constant_dynamic-update-slice_fusion.20
  658.6 0.9 constant_dynamic-update-slice_fusion.19
  659.5 0.9 constant_dynamic-update-slice_fusion.18
  660.4 0.9 constant_dynamic-update-slice_fusion.17
  661.4 0.9 constant_dynamic-update-slice_fusion.16
  662.7 3.2 copy.15
  666.0 1.0 copy.18
  667.1 1.9 copy-done.2
  669.0 2.1 fusion
  671.2 1.0 maximum_bitcast_fusion
  672.2 6.6 reshape.195
  678.8 12.9 %reduce-scatter.2.cloned.1.call-done = bf16[256,256]{0,1:T(8,128)(2,1)} async-done(((bf16[256,1024]{0,1:T(8,128)(2,1)}), bf16[256,256]{0,1:T(8,128)(2,1)}) %reduce-scatter.2.cloned.1.call-update) | async-done | bytes 131088 | tf_op jit(solution)/shard_map/reduce_scatter | solution.py:113
  691.7 1.7 copy.16
  (116 shorter events, 13.0 us)
Async XLA Ops:
  7.2 6.0 copy-start
  7.2 640.1 %all-reduce.4.cloned.1.call-start = ((), (), s32[]{:S(2)}) async-start(), calls=%async_computation.2 | async-start | bytes 8388608 | tf_op jit(solution)/shard_map/psum | solution.py:13
  18.9 328.1 %copy-start.3 = (f32[1,1,4,256,256]{4,3,2,1,0:T(8,128)S(1)}, f32[1,1,4,256,256]{4,3,2,1,0:T(8,128)}, u32[]{:S(2)}) copy-start(f32[1,1,4,256,256]{4,3,2,1,0:T(8,128)} %param.9) | copy-start | bytes 3145732
  419.8 5.3 copy-start.21
  425.4 5.3 copy-start.22
  429.4 5.3 copy-start.23
  480.9 210.8 %reduce-scatter.2.cloned.1.call-start = ((), (), s32[]{:S(2)}) async-start(), calls=%async_computation.1 | async-start | bytes 655360 | tf_op jit(solution)/shard_map/reduce_scatter | solution.py:113
  647.3 15.0 %copy-start.19 = (bf16[1,256,256]{2,1,0:T(8,128)(2,1)S(1)}, bf16[1,256,256]{2,1,0:T(8,128)(2,1)}, u32[]{:S(2)}) copy-start(bf16[1,256,256]{2,1,0:T(8,128)(2,1)} %get-tuple-element.25) | copy-start | bytes 393220
  647.3 15.0 %copy-start.18 = (bf16[1,256,256]{2,1,0:T(8,128)(2,1)S(1)}, bf16[1,256,256]{2,1,0:T(8,128)(2,1)}, u32[]{:S(2)}) copy-start(bf16[1,256,256]{2,1,0:T(8,128)(2,1)} %get-tuple-element.26) | copy-start | bytes 393220
  647.3 15.0 %copy-start.17 = (bf16[1,256,256]{2,1,0:T(8,128)(2,1)S(1)}, bf16[1,256,256]{2,1,0:T(8,128)(2,1)}, u32[]{:S(2)}) copy-start(bf16[1,256,256]{2,1,0:T(8,128)(2,1)} %get-tuple-element.27) | copy-start | bytes 393220
  647.3 15.0 %copy-start.16 = (bf16[1,256,256]{2,1,0:T(8,128)(2,1)S(1)}, bf16[1,256,256]{2,1,0:T(8,128)(2,1)}, u32[]{:S(2)}) copy-start(bf16[1,256,256]{2,1,0:T(8,128)(2,1)} %get-tuple-element.28) | copy-start | bytes 393220
  647.3 15.1 %copy-start.15 = (bf16[1,256,256]{2,1,0:T(8,128)(2,1)S(1)}, bf16[1,256,256]{2,1,0:T(8,128)(2,1)}, u32[]{:S(2)}) copy-start(bf16[1,256,256]{2,1,0:T(8,128)(2,1)} %get-tuple-element.29) | copy-start | bytes 393220
  647.3 15.1 %copy-start.14 = (bf16[1,256,256]{2,1,0:T(8,128)(2,1)S(1)}, bf16[1,256,256]{2,1,0:T(8,128)(2,1)}, u32[]{:S(2)}) copy-start(bf16[1,256,256]{2,1,0:T(8,128)(2,1)} %get-tuple-element.30) | copy-start | bytes 393220
  647.3 15.1 %copy-start.13 = (bf16[1,256,256]{2,1,0:T(8,128)(2,1)S(1)}, bf16[1,256,256]{2,1,0:T(8,128)(2,1)}, u32[]{:S(2)}) copy-start(bf16[1,256,256]{2,1,0:T(8,128)(2,1)} %get-tuple-element.31) | copy-start | bytes 393220
  647.3 15.1 %copy-start.12 = (bf16[1,256,256]{2,1,0:T(8,128)(2,1)S(1)}, bf16[1,256,256]{2,1,0:T(8,128)(2,1)}, u32[]{:S(2)}) copy-start(bf16[1,256,256]{2,1,0:T(8,128)(2,1)} %get-tuple-element.32) | copy-start | bytes 393220
  647.4 15.2 %copy-start.11 = (bf16[1,256,256]{2,1,0:T(8,128)(2,1)S(1)}, bf16[1,256,256]{2,1,0:T(8,128)(2,1)}, u32[]{:S(2)}) copy-start(bf16[1,256,256]{2,1,0:T(8,128)(2,1)} %get-tuple-element.33) | copy-start | bytes 393220
  647.4 15.2 %copy-start.10 = (bf16[1,256,256]{2,1,0:T(8,128)(2,1)S(1)}, bf16[1,256,256]{2,1,0:T(8,128)(2,1)}, u32[]{:S(2)}) copy-start(bf16[1,256,256]{2,1,0:T(8,128)(2,1)} %get-tuple-element.34) | copy-start | bytes 393220
  647.4 15.2 %copy-start.9 = (bf16[1,256,256]{2,1,0:T(8,128)(2,1)S(1)}, bf16[1,256,256]{2,1,0:T(8,128)(2,1)}, u32[]{:S(2)}) copy-start(bf16[1,256,256]{2,1,0:T(8,128)(2,1)} %get-tuple-element.35) | copy-start | bytes 393220
  647.4 15.2 %copy-start.8 = (bf16[1,256,256]{2,1,0:T(8,128)(2,1)S(1)}, bf16[1,256,256]{2,1,0:T(8,128)(2,1)}, u32[]{:S(2)}) copy-start(bf16[1,256,256]{2,1,0:T(8,128)(2,1)} %get-tuple-element.36) | copy-start | bytes 393220
  647.4 15.2 %copy-start.7 = (bf16[1,256,256]{2,1,0:T(8,128)(2,1)S(1)}, bf16[1,256,256]{2,1,0:T(8,128)(2,1)}, u32[]{:S(2)}) copy-start(bf16[1,256,256]{2,1,0:T(8,128)(2,1)} %get-tuple-element.37) | copy-start | bytes 393220
  647.4 15.2 %copy-start.6 = (bf16[1,256,256]{2,1,0:T(8,128)(2,1)S(1)}, bf16[1,256,256]{2,1,0:T(8,128)(2,1)}, u32[]{:S(2)}) copy-start(bf16[1,256,256]{2,1,0:T(8,128)(2,1)} %get-tuple-element.38) | copy-start | bytes 393220
  647.4 15.3 %copy-start.5 = (bf16[1,256,256]{2,1,0:T(8,128)(2,1)S(1)}, bf16[1,256,256]{2,1,0:T(8,128)(2,1)}, u32[]{:S(2)}) copy-start(bf16[1,256,256]{2,1,0:T(8,128)(2,1)} %get-tuple-element.39) | copy-start | bytes 393220
  647.4 15.3 %copy-start.4 = (bf16[1,256,256]{2,1,0:T(8,128)(2,1)S(1)}, bf16[1,256,256]{2,1,0:T(8,128)(2,1)}, u32[]{:S(2)}) copy-start(bf16[1,256,256]{2,1,0:T(8,128)(2,1)} %get-tuple-element.40) | copy-start | bytes 393220
  666.0 3.0 copy-start.20
  667.0 1.9 copy-start.2
  671.1 22.2 %copy-start.1 = (bf16[256,2048]{1,0:T(8,128)(2,1)S(1)}, bf16[256,2048]{1,0:T(8,128)(2,1)}, u32[]{:S(2)}) copy-start(bf16[256,2048]{1,0:T(8,128)(2,1)} %param.6) | copy-start | bytes 3145732
Sparse Core Ops, SparseCore 0:
  481.0 166.2 all-reduce.3
  671.3 20.4 reduce-scatter.1
where the time goes:
time: 702 us; the launch traced here: 700 us
  blocking collectives  328 us (47%)
  waiting for transfers between devices  179 us (25%)
  between operations  108 us (15%)
  matrix products  40.3 us (6%)
  local copies, waits for them, and re-layouts  27 us (4%)
  other arithmetic  17.4 us (2%)
    psum x1, blocking collectives, body(): summed = lax.psum(partial_grad, 'dp')  328 us
    psum x1, waiting for transfers between devices, from_root(): return lax.psum(jnp.where(mine, x, jnp.zeros_like(x)), axis)  166 us
    unnamed x82, local copies, waits for them, and re-layouts  19.8 us
  transfers between devices with their start and end apart: 2, of which 2 were waited for; matrix products, arithmetic and copies ran while one was open for 1% of the time, Pallas kernels for 0%

commit v1 on v0

--- a/solution.py
+++ b/solution.py
@@ -61,7 +61,9 @@
     partial_grad = jnp.einsum(
         "td,tc->dc", activations, cotangent, preferred_element_type=jnp.float32
     )
-    summed = lax.psum(partial_grad, "dp")
+    summed = partial_grad
+    for hop in (1, 2, 4):
+        summed = summed + lax.ppermute(summed, "dp", [(dev, dev ^ hop) for dev in range(8)])
     grad_low = summed.astype(jnp.bfloat16)
     feat_index = lax.axis_index("feat")
     data_index = lax.axis_index("dp")

time: 702 us -> 1050 us (1.50)
  waiting for transfers between devices: 179 us -> 805 us
  blocking collectives: 328 us -> 0 us
  other arithmetic: 17.4 us -> 49.1 us
    ppermute x0 -> x3, waiting for transfers between devices: none -> 624 us  [body(): lax.ppermute(summed, 'dp', [(dev, dev ^ hop) for dev in range(8)])]
    psum x1 -> x0, blocking collectives: 328 us -> none  [body(): summed = lax.psum(partial_grad, 'dp')]
    add x0 -> x2, other arithmetic: none -> 24.3 us  [body(): summed + lax.ppermute(summed, 'dp', [(dev, dev ^ hop) for dev in range(8)])]
    unnamed x82 -> x86, local copies, waits for them, and re-layouts: 19.8 us -> 26.4 us
  transfers between devices with their start and end apart: 2 -> 5, of which waited for: 2 -> 5; matrix products, arithmetic and copies ran while one was open for 1% -> 1% of each run, Pallas kernels for 0% -> 0%
where the time goes in v1:
time: 1050 us; the launch traced here: 1040 us
  waiting for transfers between devices  805 us (77%)
  between operations  108 us (10%)
  other arithmetic  49.1 us (5%)
  matrix products  41.9 us (4%)
  local copies, waits for them, and re-layouts  32.8 us (3%)
    ppermute x3, waiting for transfers between devices, body(): lax.ppermute(summed, 'dp', [(dev, dev ^ hop) for dev in range(8)])  624 us
    psum x1, waiting for transfers between devices, from_root(): return lax.psum(jnp.where(mine, x, jnp.zeros_like(x)), axis)  169 us
    unnamed x86, local copies, waits for them, and re-layouts  26.4 us
    add x2, other arithmetic, body(): summed + lax.ppermute(summed, 'dp', [(dev, dev ^ hop) for dev in range(8)])  24.3 us
  transfers between devices with their start and end apart: 5, of which 5 were waited for; matrix products, arithmetic and copies ran while one was open for 1% of the time, Pallas kernels for 0%

profile of v1, /device:TPU:0, one launch (start us, length us, event | category | flops | bytes accessed | tf_op | source)
XLA Modules:
  0.0 1044.4 jit_solution(18159380219347900814)
XLA Ops:
  7.2 1.2 copy-done
  8.4 2.3 fusion.363
  10.7 3.4 copy-done.2
  14.1 3.0 collective-permute-start
  17.1 180.6 %collective-permute-done = f32[2048,1024]{1,0:T(8,128)} collective-permute-done((f32[2048,1024]{1,0:T(8,128)S(1)}, f32[2048,1024]{1,0:T(8,128)}, u32[]{:S(2)}, u32[]{:S(2)}) %collective-permute-start) | collective-permute-done | bytes 8388640 | tf_op jit(solution)/shard_map/ppermute | solution.py:66
  197.7 12.1 %add.272 = f32[2048,1024]{1,0:T(8,128)} add(f32[2048,1024]{1,0:T(8,128)} %copy-done.2, f32[2048,1024]{1,0:T(8,128)} %collective-permute-done) | non-fusion elementwise | flops 2097152 | bytes 25165824 | tf_op jit(solution)/shard_map/add | solution.py:66
  209.8 1.8 collective-permute-start.1
  211.6 180.1 %collective-permute-done.1 = f32[2048,1024]{1,0:T(8,128)} collective-permute-done((f32[2048,1024]{1,0:T(8,128)}, f32[2048,1024]{1,0:T(8,128)}, u32[]{:S(2)}, u32[]{:S(2)}) %collective-permute-start.1) | collective-permute-done | bytes 8388640 | tf_op jit(solution)/shard_map/ppermute | solution.py:66
  391.7 12.1 %add.273 = f32[2048,1024]{1,0:T(8,128)} add(f32[2048,1024]{1,0:T(8,128)} %add.272, f32[2048,1024]{1,0:T(8,128)} %collective-permute-done.1) | non-fusion elementwise | flops 2097152 | bytes 25165824 | tf_op jit(solution)/shard_map/add | solution.py:66
  403.9 2.6 collective-permute-start.2
  427.6 0.7 fusion.360
  465.3 0.7 fusion.359
  502.7 263.0 %collective-permute-done.2 = f32[2048,1024]{1,0:T(8,128)} collective-permute-done((f32[2048,1024]{1,0:T(8,128)}, f32[2048,1024]{1,0:T(8,128)}, u32[]{:S(2)}, u32[]{:S(2)}) %collective-permute-start.2) | collective-permute-done | bytes 8388640 | tf_op jit(solution)/shard_map/ppermute | solution.py:66
  765.6 7.3 add_convert_fusion
  772.9 2.0 copy-done.4
  774.9 0.9 multiply_reduce_fusion
  777.9 1.1 convolution_convert_fusion.10
  779.0 1.0 convolution_convert_fusion.12
  779.9 1.9 multiply_reduce_fusion.1
  783.8 1.1 convolution_convert_fusion.25
  784.9 1.0 convolution_convert_fusion.27
  786.0 1.9 multiply_reduce_fusion.2
  790.4 1.0 convolution_convert_fusion.42
  791.5 1.9 multiply_reduce_fusion.3
  794.1 0.7 select_bitcast_fusion.3
  796.1 1.0 convolution_convert_fusion.57
  797.2 1.1 fusion.102
  800.2 1.2 convolution_convert_fusion.6
  803.6 1.9 convolution_convert_fusion.21
  805.8 1.2 fusion.2
  807.1 1.2 fusion.22
  808.3 1.2 fusion.6
  811.7 1.2 convolution_convert_fusion.36
  813.3 1.2 fusion.10
  817.3 1.2 fusion.14
  818.6 0.8 fusion.69
  819.5 1.1 fusion.78
  820.5 1.1 fusion.87
  821.6 1.1 fusion.96
  822.9 168.5 %all-reduce.3.cloned.1.call-done = (bf16[1,256,256]{2,1,0:T(8,128)(2,1)}, bf16[1,256,256]{2,1,0:T(8,128)(2,1)}, bf16[1,256,256]{2,1,0:T(8,128)(2,1)}, bf16[1,256...) async-done(((bf16[1,256,256]{2,1,0:T(8,128)(2,1)}, ...) | async-done | bytes 4194320 | tf_op jit(solution)/shard_map/psum | solution.py:13
  991.6 1.1 constant_dynamic-update-slice_fusion.31
  992.7 0.9 constant_dynamic-update-slice_fusion.30
  993.6 0.9 constant_dynamic-update-slice_fusion.29
  994.5 0.9 constant_dynamic-update-slice_fusion.28
  995.4 0.9 constant_dynamic-update-slice_fusion.27
  996.3 0.9 constant_dynamic-update-slice_fusion.26
  997.3 0.9 constant_dynamic-update-slice_fusion.25
  998.2 0.9 constant_dynamic-update-slice_fusion.24
  999.1 0.9 constant_dynamic-update-slice_fusion.23
  1000.0 0.9 constant_dynamic-update-slice_fusion.22
  1000.9 0.9 constant_dynamic-update-slice_fusion.21
  1001.8 0.9 constant_dynamic-update-slice_fusion.20
  1002.8 0.9 constant_dynamic-update-slice_fusion.19
  1003.7 0.9 constant_dynamic-update-slice_fusion.18
  1004.6 0.9 constant_dynamic-update-slice_fusion.17
  1005.5 0.9 constant_dynamic-update-slice_fusion.16
  1006.9 3.2 copy.15
  1010.2 1.0 copy.18
  1011.2 1.9 copy-done.3
  1013.2 2.1 fusion
  1015.3 1.0 maximum_bitcast_fusion
  1016.4 6.6 reshape.195
  1023.0 12.9 %reduce-scatter.2.cloned.1.call-done = bf16[256,256]{0,1:T(8,128)(2,1)} async-done(((bf16[256,1024]{0,1:T(8,128)(2,1)}), bf16[256,256]{0,1:T(8,128)(2,1)}) %reduce-scatter.2.cloned.1.call-update) | async-done | bytes 131088 | tf_op jit(solution)/shard_map/reduce_scatter | solution.py:115
  1035.9 1.7 copy.16
  (128 shorter events, 20.6 us)
Async XLA Ops:
  7.2 1.2 copy-start
  7.2 984.3 %all-reduce.3.cloned.1.call-start = ((), (), s32[]{:S(2)}) async-start(), calls=%async_computation.2 | async-start | bytes 8388608 | tf_op jit(solution)/shard_map/psum | solution.py:13
  10.7 3.4 copy-start.2
  14.1 183.5 %collective-permute-start = (f32[2048,1024]{1,0:T(8,128)S(1)}, f32[2048,1024]{1,0:T(8,128)}, u32[]{:S(2)}, u32[]{:S(2)}) collective-permute-start(f32[2048,1024]{1,0:T(8,128)S(1)} %fusion.363), channel_id=1, source_target_pairs={{0,4},{4,0},{8,12},{12,8},{16,20},{20,16},{24,28},{28,24},{1,5},{5... | collective-permute-start | bytes 25165832 | tf_op jit(solution)/shard_map/ppermute | solution.py:66
  209.8 196.6 %copy-start.23 = (s32[32,4]{0,1:T(4,128)S(1)}, s32[32,4]{0,1:T(4,128)}, u32[]{:S(2)}) copy-start(s32[32,4]{0,1:T(4,128)} %param.10) | copy-start | bytes 1540
  209.8 181.9 %collective-permute-start.1 = (f32[2048,1024]{1,0:T(8,128)}, f32[2048,1024]{1,0:T(8,128)}, u32[]{:S(2)}, u32[]{:S(2)}) collective-permute-start(f32[2048,1024]{1,0:T(8,128)} %add.272), channel_id=1, source_target_pairs={{0,8},{4,12},{8,0},{12,4},{16,24},{20,28},{24,16},{28,20},{1,9},{5... | collective-permute-start | bytes 25165832 | tf_op jit(solution)/shard_map/ppermute | solution.py:66
  403.9 361.7 %collective-permute-start.2 = (f32[2048,1024]{1,0:T(8,128)}, f32[2048,1024]{1,0:T(8,128)}, u32[]{:S(2)}, u32[]{:S(2)}) collective-permute-start(f32[2048,1024]{1,0:T(8,128)} %add.273), channel_id=1, source_target_pairs={{0,16},{4,20},{8,24},{12,28},{16,0},{20,4},{24,8},{28,12},{1,17},{... | collective-permute-start | bytes 25165832 | tf_op jit(solution)/shard_map/ppermute | solution.py:66
  502.7 272.3 %copy-start.5 = (f32[1,1,4,256,256]{4,3,2,1,0:T(8,128)S(1)}, f32[1,1,4,256,256]{4,3,2,1,0:T(8,128)}, u32[]{:S(2)}) copy-start(f32[1,1,4,256,256]{4,3,2,1,0:T(8,128)} %param.9) | copy-start | bytes 3145732
  772.9 2.0 copy-start.4
  793.4 8.1 copy-start.6
  810.4 6.2 copy-start.25
  822.7 213.2 %reduce-scatter.2.cloned.1.call-start = ((), (), s32[]{:S(2)}) async-start(), calls=%async_computation.1 | async-start | bytes 655360 | tf_op jit(solution)/shard_map/reduce_scatter | solution.py:115
  991.5 15.0 %copy-start.22 = (bf16[1,256,256]{2,1,0:T(8,128)(2,1)S(1)}, bf16[1,256,256]{2,1,0:T(8,128)(2,1)}, u32[]{:S(2)}) copy-start(bf16[1,256,256]{2,1,0:T(8,128)(2,1)} %get-tuple-element.25) | copy-start | bytes 393220
  991.5 15.0 %copy-start.21 = (bf16[1,256,256]{2,1,0:T(8,128)(2,1)S(1)}, bf16[1,256,256]{2,1,0:T(8,128)(2,1)}, u32[]{:S(2)}) copy-start(bf16[1,256,256]{2,1,0:T(8,128)(2,1)} %get-tuple-element.26) | copy-start | bytes 393220
  991.5 15.0 %copy-start.20 = (bf16[1,256,256]{2,1,0:T(8,128)(2,1)S(1)}, bf16[1,256,256]{2,1,0:T(8,128)(2,1)}, u32[]{:S(2)}) copy-start(bf16[1,256,256]{2,1,0:T(8,128)(2,1)} %get-tuple-element.27) | copy-start | bytes 393220
  991.5 15.0 %copy-start.19 = (bf16[1,256,256]{2,1,0:T(8,128)(2,1)S(1)}, bf16[1,256,256]{2,1,0:T(8,128)(2,1)}, u32[]{:S(2)}) copy-start(bf16[1,256,256]{2,1,0:T(8,128)(2,1)} %get-tuple-element.28) | copy-start | bytes 393220
  991.5 15.1 %copy-start.18 = (bf16[1,256,256]{2,1,0:T(8,128)(2,1)S(1)}, bf16[1,256,256]{2,1,0:T(8,128)(2,1)}, u32[]{:S(2)}) copy-start(bf16[1,256,256]{2,1,0:T(8,128)(2,1)} %get-tuple-element.29) | copy-start | bytes 393220
  991.5 15.1 %copy-start.17 = (bf16[1,256,256]{2,1,0:T(8,128)(2,1)S(1)}, bf16[1,256,256]{2,1,0:T(8,128)(2,1)}, u32[]{:S(2)}) copy-start(bf16[1,256,256]{2,1,0:T(8,128)(2,1)} %get-tuple-element.30) | copy-start | bytes 393220
  991.5 15.1 %copy-start.16 = (bf16[1,256,256]{2,1,0:T(8,128)(2,1)S(1)}, bf16[1,256,256]{2,1,0:T(8,128)(2,1)}, u32[]{:S(2)}) copy-start(bf16[1,256,256]{2,1,0:T(8,128)(2,1)} %get-tuple-element.31) | copy-start | bytes 393220
  991.5 15.1 %copy-start.15 = (bf16[1,256,256]{2,1,0:T(8,128)(2,1)S(1)}, bf16[1,256,256]{2,1,0:T(8,128)(2,1)}, u32[]{:S(2)}) copy-start(bf16[1,256,256]{2,1,0:T(8,128)(2,1)} %get-tuple-element.32) | copy-start | bytes 393220
  991.5 15.2 %copy-start.14 = (bf16[1,256,256]{2,1,0:T(8,128)(2,1)S(1)}, bf16[1,256,256]{2,1,0:T(8,128)(2,1)}, u32[]{:S(2)}) copy-start(bf16[1,256,256]{2,1,0:T(8,128)(2,1)} %get-tuple-element.33) | copy-start | bytes 393220
  991.5 15.2 %copy-start.13 = (bf16[1,256,256]{2,1,0:T(8,128)(2,1)S(1)}, bf16[1,256,256]{2,1,0:T(8,128)(2,1)}, u32[]{:S(2)}) copy-start(bf16[1,256,256]{2,1,0:T(8,128)(2,1)} %get-tuple-element.34) | copy-start | bytes 393220
  991.5 15.2 %copy-start.12 = (bf16[1,256,256]{2,1,0:T(8,128)(2,1)S(1)}, bf16[1,256,256]{2,1,0:T(8,128)(2,1)}, u32[]{:S(2)}) copy-start(bf16[1,256,256]{2,1,0:T(8,128)(2,1)} %get-tuple-element.35) | copy-start | bytes 393220
  991.5 15.2 %copy-start.11 = (bf16[1,256,256]{2,1,0:T(8,128)(2,1)S(1)}, bf16[1,256,256]{2,1,0:T(8,128)(2,1)}, u32[]{:S(2)}) copy-start(bf16[1,256,256]{2,1,0:T(8,128)(2,1)} %get-tuple-element.36) | copy-start | bytes 393220
  991.6 15.2 %copy-start.10 = (bf16[1,256,256]{2,1,0:T(8,128)(2,1)S(1)}, bf16[1,256,256]{2,1,0:T(8,128)(2,1)}, u32[]{:S(2)}) copy-start(bf16[1,256,256]{2,1,0:T(8,128)(2,1)} %get-tuple-element.37) | copy-start | bytes 393220
  991.6 15.2 %copy-start.9 = (bf16[1,256,256]{2,1,0:T(8,128)(2,1)S(1)}, bf16[1,256,256]{2,1,0:T(8,128)(2,1)}, u32[]{:S(2)}) copy-start(bf16[1,256,256]{2,1,0:T(8,128)(2,1)} %get-tuple-element.38) | copy-start | bytes 393220
  991.6 15.3 %copy-start.8 = (bf16[1,256,256]{2,1,0:T(8,128)(2,1)S(1)}, bf16[1,256,256]{2,1,0:T(8,128)(2,1)}, u32[]{:S(2)}) copy-start(bf16[1,256,256]{2,1,0:T(8,128)(2,1)} %get-tuple-element.39) | copy-start | bytes 393220
  991.6 15.3 %copy-start.7 = (bf16[1,256,256]{2,1,0:T(8,128)(2,1)S(1)}, bf16[1,256,256]{2,1,0:T(8,128)(2,1)}, u32[]{:S(2)}) copy-start(bf16[1,256,256]{2,1,0:T(8,128)(2,1)} %get-tuple-element.40) | copy-start | bytes 393220
  1010.1 3.0 copy-start.24
  1011.2 1.9 copy-start.3
  1015.3 22.2 %copy-start.1 = (bf16[256,2048]{1,0:T(8,128)(2,1)S(1)}, bf16[256,2048]{1,0:T(8,128)(2,1)}, u32[]{:S(2)}) copy-start(bf16[256,2048]{1,0:T(8,128)(2,1)} %param.6) | copy-start | bytes 3145732
Sparse Core Ops, SparseCore 0:
  822.8 168.6 all-reduce.2
  1015.4 20.4 reduce-scatter.1
